TPU v7x, 32 devices: a whole 2x2x4 slice. The times are simulated.
32 devices in a mesh: tm: 8 (over z, y), env: 4 (over x, core).
Axes of the slice: x: 2, y: 2, z: 4, core: 2. Of those that a mesh axis runs over, the one named last changes fastest.
Arguments:
- rewards: float32 [16384, 2048], P('tm', 'env'), may hold values from -0.16 to 0.16
- values: float32 [16384, 2048], P('tm', 'env'), may hold values from -6 to 6
- last_value: float32 [2048], P('env'), may hold values from -6 to 6
- done_steps: int32 [2048, 4], P('env'), may hold values from 0 to 16383
- horizon_offset: int32 [2048], P('env'), may hold values from 0 to 8191
- discount_rate: float32 [2048], P('env'), may hold values from 3.0517579e-06 to 0.03
- trace_rate: float32 [2048], P('env'), may hold values from 3.0517579e-06 to 0.03
Outputs:
- norm_advantages: float32 [2048, 16384], P(('env', 'tm'))
- norm_returns: float32 [2048, 16384], P(('env', 'tm'))
Inputs may be any that keep to these rules, and one draw needn't show every extreme that they name: `done_steps`: a repeated step in one environment's list is one termination.
All inputs are finite; a program needn't handle non-finite values.
Results may differ from a plain program's by a relative error of at most 0.0008.
Values sent between devices are 32-bit elements; how exact they have to be, the bound alone decides.
A program may use at most 128 MiB of HBM per device.

v0:
```python
import functools

import jax
import jax.numpy as jnp
from jax import lax
from jax.experimental import pallas as pl
from jax.experimental.pallas import tpu as pltpu
from jax.sharding import PartitionSpec as P

MESH = pl.DeviceIdType.MESH
CHUNKS = 4
SIDE = 128


def combine(parts):
    count = len(parts)
    means = [part[0:2] for part in parts]
    mean = functools.reduce(jnp.add, means) / count
    spread = [part[2:4] + (m - mean) * (m - mean) for part, m in zip(parts, means)]
    return mean, functools.reduce(jnp.add, spread) / count


def exchange(
    n, m, horizon, samples,
    rewards, values, last, done, offset, rate_d, rate_t,
    out_a, out_v,
    p_buf, v_buf, d_buf, vt, at, src, summary, st_one, env_stats, st_two, tm_stats,
    load_r, load_v, send_big, recv_v, recv_a, send_sum, recv_sum,
    send_env, recv_env, send_tm, recv_tm,
):
    steps, envs = v_buf.shape
    rows = envs // n
    part = steps // CHUNKS
    me = lax.axis_index("tm")
    my_env = lax.axis_index("env")
    links = [(lax.rem(me + d, n), lax.rem(me + n - d, n)) for d in range(1, n)]
    peers = [target for target, unused in links]
    mates = [lax.rem(my_env + d, m) for d in range(1, m)]

    loads_v = [
        pltpu.make_async_copy(
            values.at[pl.ds(c * part, part)], v_buf.at[pl.ds(c * part, part)], load_v.at[c]
        )
        for c in range(CHUNKS)
    ]
    loading_r = pltpu.make_async_copy(rewards, p_buf, load_r)
    for load in loads_v:
        load.start()
    loading_r.start()

    barrier = pltpu.get_barrier_semaphore()
    for peer in peers:
        pl.semaphore_signal(barrier, inc=1, device_id={"tm": peer}, device_id_type=MESH)
    for mate in mates:
        pl.semaphore_signal(barrier, inc=1, device_id={"env": mate}, device_id_type=MESH)
    pl.semaphore_wait(barrier, n + m - 2)

    def send_part(which, source, target, sems, first, width, places):
        for place in places:
            peer = links[place][0]
            pltpu.make_async_remote_copy(
                src_ref=source.at[
                    pl.ds(pl.multiple_of(peer * rows, 8), rows), pl.ds(first, width)
                ],
                dst_ref=target.at[
                    pl.ds(0, rows), pl.ds(pl.multiple_of(me * steps + first, SIDE), width)
                ],
                send_sem=send_big.at[which],
                recv_sem=sems(place),
                device_id={"tm": peer},
                device_id_type=MESH,
            ).start()

    everyone = range(n - 1)

    def send_values(first, width):
        send_part(0, vt, out_v, lambda place: recv_v.at[place], first, width, everyone)

    def send_advantages(c, places):
        sems = lambda place: recv_a.at[place * CHUNKS + c]
        send_part(1, at, out_a, sems, c * part, part, places)

    def turn_values(first, width):
        def body(b, unused):
            t = pl.multiple_of(first + b * SIDE, SIDE)
            for e in range(0, envs, SIDE):
                vt[pl.ds(e, SIDE), pl.ds(t, SIDE)] = v_buf[pl.ds(t, SIDE), pl.ds(e, SIDE)].T
            return unused

        lax.fori_loop(0, width // SIDE, body, 0)

    half = CHUNKS // 2
    loads_v[0].wait()
    turn_values(0, SIDE)
    send_values(0, SIDE)
    turn_values(SIDE, part - SIDE)
    send_values(SIDE, part - SIDE)
    for c in range(1, half):
        loads_v[c].wait()
        turn_values(c * part, part)
        send_values(c * part, part)
    for c in range(half, CHUNKS):
        loads_v[c].wait()
    loading_r.wait()

    discount = jnp.exp(-rate_d[...])
    retention = discount * jnp.exp(-rate_t[...])
    first = me * steps
    wide = (8, envs)
    ends = [jnp.broadcast_to(done[j : j + 1, :] - first, wide) for j in range(done.shape[0])]
    cuts = [
        jnp.broadcast_to(k * horizon - 1 - first - offset[...], wide)
        for k in (1, 2)
    ]
    disc = jnp.broadcast_to(discount, wide)
    keep = jnp.broadcast_to(retention, wide)
    row = lax.broadcasted_iota(jnp.int32, wide, 0)

    def tile(k, later, final):
        v_later, a_later, d_later = later
        at_rows = pl.ds(pl.multiple_of(k * 8, 8), 8)
        v = v_buf[at_rows, :]
        r = p_buf[at_rows, :]
        moment = row + k * 8
        finished = functools.reduce(jnp.logical_or, [moment == e for e in ends])
        stopped = functools.reduce(jnp.logical_or, [moment == e for e in cuts], finished)
        reach = jnp.where(finished, 0.0, disc)
        decay = jnp.where(stopped, 0.0, keep)
        v_up = pltpu.roll(v, 7, 0)
        if final:
            src[3:4, :] = reach[7:8, :]
            src[4:5, :] = decay[7:8, :]
            td = r + jnp.where(row == 7, 0.0, reach * v_up) - v
            decay = jnp.where(row == 7, 1.0, decay)
        else:
            td = r + reach * jnp.where(row == 7, v_later, v_up) - v
        for s in (1, 2, 4):
            inside = row < 8 - s
            td_up = jnp.where(inside, pltpu.roll(td, 8 - s, 0), 0.0)
            decay_up = jnp.where(inside, pltpu.roll(decay, 8 - s, 0), 1.0)
            td = td + decay * td_up
            decay = decay * decay_up
        if not final:
            td = td + decay * a_later
            decay = decay * d_later
        p_buf[at_rows, :] = td
        d_buf[at_rows, :] = decay
        return (
            v_up,
            jnp.broadcast_to(td[0:1, :], wide),
            jnp.broadcast_to(decay[0:1, :], wide),
        )

    tiles = steps // 8
    state = tile(tiles - 1, (None, None, None), True)
    lax.fori_loop(0, tiles - 1, lambda i, s: tile(tiles - 2 - i, s, False), state)

    src[0:1, :] = p_buf[0:1, :]
    src[1:2, :] = d_buf[0:1, :]
    src[2:3, :] = v_buf[0:1, :]
    src[5:8, :] = jnp.zeros((3, envs), jnp.float32)
    turn_values(half * part, steps - half * part)
    summary[me] = src[...]
    for peer in peers:
        pltpu.make_async_remote_copy(
            src_ref=src, dst_ref=summary.at[me], send_sem=send_sum, recv_sem=recv_sum,
            device_id={"tm": peer}, device_id_type=MESH,
        ).start()
    for c in range(half, CHUNKS):
        send_values(c * part, part)

    def wait_all(source_like, sem):
        pltpu.make_async_copy(source_like, source_like, sem).wait()

    others = summary.at[pl.ds(0, n - 1)]
    wait_all(others, recv_sum)

    a_next = jnp.zeros((1, envs), jnp.float32)
    v_next = last[...]
    lift = jnp.zeros((1, envs), jnp.float32)
    for p in reversed(range(n)):
        block = summary[p]
        added = block[3:4] * v_next + block[4:5] * a_next
        lift = jnp.where(me == p, added, lift)
        a_next = block[0:1] + block[1:2] * added
        v_next = block[2:3]
    src_lift = [jnp.broadcast_to(lift[:, e : e + SIDE], (SIDE, SIDE)) for e in range(0, envs, SIDE)]

    def fold(x):
        return jnp.sum(x.reshape(SIDE // 8, 8, SIDE), axis=0)

    def finish(b, sums):
        sum_a, sum_v = sums
        t = pl.multiple_of(b * SIDE, SIDE)
        for i, e in enumerate(range(0, envs, SIDE)):
            here = (pl.ds(t, SIDE), pl.ds(e, SIDE))
            a = p_buf[here] + d_buf[here] * src_lift[i]
            at[pl.ds(e, SIDE), pl.ds(t, SIDE)] = a.T
            sum_a = sum_a + fold(a)
            sum_v = sum_v + fold(v_buf[here])
        return sum_a, sum_v

    zero = jnp.zeros((8, SIDE), jnp.float32)
    sum_a, sum_v = lax.fori_loop(0, steps // SIDE, finish, (zero, zero))
    total = lambda x: jnp.sum(jnp.sum(x, axis=1, keepdims=True), axis=0, keepdims=True)
    mean_a = total(sum_a) / samples
    mean_r = mean_a + total(sum_v) / samples
    span = 4 * SIDE
    mid_a = jnp.broadcast_to(mean_a, (8, span))
    mid_r = jnp.broadcast_to(mean_r, (8, span))

    def squares(i, sums):
        sq_a, sq_r = sums
        for t in range(0, steps, span):
            here = (pl.ds(pl.multiple_of(i * 8, 8), 8), pl.ds(t, span))
            a = at[here]
            dev_a = a - mid_a
            dev_r = (a + vt[here]) - mid_r
            sq_a = sq_a + dev_a * dev_a
            sq_r = sq_r + dev_r * dev_r
        return sq_a, sq_r

    zero = jnp.zeros((8, span), jnp.float32)
    sq_a, sq_r = lax.fori_loop(0, envs // 8, squares, (zero, zero))
    lane = (1, SIDE)
    st_one[0:1, :] = jnp.broadcast_to(mean_a, lane)
    st_one[1:2, :] = jnp.broadcast_to(mean_r, lane)
    st_one[2:3, :] = jnp.broadcast_to(total(sq_a) / samples, lane)
    st_one[3:4, :] = jnp.broadcast_to(total(sq_r) / samples, lane)
    st_one[4:8, :] = jnp.zeros((4, SIDE), jnp.float32)
    env_stats[my_env] = st_one[...]

    for mate in mates:
        pltpu.make_async_remote_copy(
            src_ref=st_one, dst_ref=env_stats.at[my_env], send_sem=send_env, recv_sem=recv_env,
            device_id={"env": mate}, device_id_type=MESH,
        ).start()
    send_advantages(0, everyone)
    send_advantages(1, everyone)
    wait_all(env_stats.at[pl.ds(0, m - 1)], recv_env)
    mean, var = combine([env_stats[q] for q in range(m)])
    st_two[0:2, :] = mean
    st_two[2:4, :] = var
    st_two[4:8, :] = jnp.zeros((4, SIDE), jnp.float32)
    tm_stats[me] = st_two[...]
    for peer in peers:
        pltpu.make_async_remote_copy(
            src_ref=st_two, dst_ref=tm_stats.at[me], send_sem=send_tm, recv_sem=recv_tm,
            device_id={"tm": peer}, device_id_type=MESH,
        ).start()
    for c in range(2, CHUNKS):
        send_advantages(c, everyone)

    wait_all(tm_stats.at[pl.ds(0, n - 1)], recv_tm)
    mean, var = combine([tm_stats[q] for q in range(n)])
    scale = lax.rsqrt(var + 1e-05)
    wide = (8, part)
    mid_a, mid_r, scale_a, scale_r = (
        jnp.broadcast_to(x[i : i + 1, 0:1], wide) for x in (mean, scale) for i in (0, 1)
    )

    def normalize(read_a, read_v, first):
        for r in range(0, rows, 8):
            here = (pl.ds(r, 8), pl.ds(first, part))
            a = read_a(r)
            v = read_v(r)
            out_a[here] = (a - mid_a) * scale_a
            out_v[here] = ((a + v) - mid_r) * scale_r

    def own(c, unused):
        def read(source):
            return lambda r: source[
                pl.ds(pl.multiple_of(me * rows + r, 8), 8),
                pl.ds(pl.multiple_of(c * part, SIDE), part),
            ]
        normalize(read(at), read(vt), pl.multiple_of(me * steps + c * part, SIDE))
        return unused

    lax.fori_loop(0, CHUNKS, own, 0)

    def arrived(place, c):
        first = pl.multiple_of(links[place][1] * steps + c * part, SIDE)
        piece = out_a.at[:, pl.ds(0, part)]
        if c == 0:
            wait_all(out_v.at[:, pl.ds(0, steps)], recv_v.at[place])
        wait_all(piece, recv_a.at[place * CHUNKS + c])
        read = lambda source: lambda r: source[pl.ds(r, 8), pl.ds(first, part)]
        normalize(read(out_a), read(out_v), first)

    for c in range(CHUNKS):
        for place in everyone:
            arrived(place, c)

    wait_all(others, send_sum)
    wait_all(env_stats.at[pl.ds(0, m - 1)], send_env)
    wait_all(tm_stats.at[pl.ds(0, n - 1)], send_tm)
    for which, source in enumerate((vt, at)):
        wait_all(source.at[pl.ds(0, (n - 1) * rows)], send_big.at[which])


def shards(rewards, values, last_value, done_steps, horizon_offset, discount_rate, trace_rate):
    steps, envs = rewards.shape
    n, m = lax.axis_size("tm"), lax.axis_size("env")
    rows = envs // n
    horizon = steps * n // 2
    whole = pltpu.VMEM((rows, steps * n), jnp.float32)
    kernel = functools.partial(exchange, n, m, horizon, float(steps * envs))
    remote = pl.BlockSpec(memory_space=pltpu.HBM)
    local = pl.BlockSpec(memory_space=pltpu.VMEM)
    f32 = jnp.float32
    dma = pltpu.SemaphoreType.DMA
    return pl.pallas_call(
        kernel,
        out_shape=(whole, whole),
        in_specs=[remote] * 2 + [local] * 5,
        out_specs=(local, local),
        scratch_shapes=[
            pltpu.VMEM((steps, envs), f32),
            pltpu.VMEM((steps, envs), f32),
            pltpu.VMEM((steps, envs), f32),
            pltpu.VMEM((envs, steps), f32),
            pltpu.VMEM((envs, steps), f32),
            pltpu.VMEM((8, envs), f32),
            pltpu.VMEM((n, 8, envs), f32),
            pltpu.VMEM((8, SIDE), f32),
            pltpu.VMEM((m, 8, SIDE), f32),
            pltpu.VMEM((8, SIDE), f32),
            pltpu.VMEM((n, 8, SIDE), f32),
            dma, dma((CHUNKS,)), dma((2,)), dma((n - 1,)), dma(((n - 1) * CHUNKS,)), dma, dma,
            dma, dma, dma, dma,
        ],
        compiler_params=pltpu.CompilerParams(
            collective_id=0, has_side_effects=True, vmem_limit_bytes=55 * 1024 * 1024
        ),
    )(
        rewards,
        values,
        last_value[None, :],
        done_steps.T,
        horizon_offset[None, :],
        discount_rate[None, :],
        trace_rate[None, :],
    )


def solution(mesh):
    in_specs = (
        P("tm", "env"),
        P("tm", "env"),
        P("env"),
        P("env", None),
        P("env"),
        P("env"),
        P("env"),
    )
    out_specs = (P(("env", "tm"), None), P(("env", "tm"), None))
    return jax.shard_map(shards, mesh=mesh, in_specs=in_specs, out_specs=out_specs, check_vma=False)
```

profile of v0, /device:TPU:15, one launch (start us, length us, event | category | flops | bytes accessed | tf_op | source)
XLA Modules:
  0.0 194.2 jit_solution(8547803493860084412)
XLA Ops:
  0.6 189.5 %shard_map.86 = (f32[64,16384]{1,0:T(8,128)S(1)}, f32[64,16384]{1,0:T(8,128)S(1)}) custom-call(f32[2048,512]{1,0:T(8,128)} %rewards.1, f32[2048,512]{1,0:T(8,128)} %values.1, f32[1,512]{1,0:T(1,128)} %bitcast.6, s32[4,512]{1,0:T(4,128)} %bitcast.5, s32[1,512]{1,0:T(1,128)} %bitcast.7, f32[1,512]{1,0:T(1,128)} %bitcast.8, f32[1,512]{1,0:T(1,128)} %bitcast.9), custom_call_target="tpu_custom_call" | custom-call | tf_op jit(solution)/shard_map/pallas_call | solution.py:312
  190.2 2.0 %copy.11 = f32[64,16384]{1,0:T(8,128)} copy(f32[64,16384]{1,0:T(8,128)S(1)} %get-tuple-element.2) | data formatting | bytes 8388608
  192.2 2.0 %copy.12 = f32[64,16384]{1,0:T(8,128)} copy(f32[64,16384]{1,0:T(8,128)S(1)} %get-tuple-element.3) | data formatting | bytes 8388608
where the time goes:
time: 194 us
  Pallas kernels  190 us (98%)
  local copies, waits for them, and re-layouts  4.03 us (2%)
    pallas_call x1, Pallas kernels, shards(): pl.pallas_call(kernel, out_shape=(whole, whole), in_specs=[remote] * 2 +...  190 us
    unnamed x2, local copies, waits for them, and re-layouts  4.03 us

commit v1 on v0

--- a/solution.py
+++ b/solution.py
@@ -10,6 +10,7 @@
 MESH = pl.DeviceIdType.MESH
 CHUNKS = 4
 SIDE = 128
+PIECES = 4
 
 
 def combine(parts):
@@ -20,65 +21,111 @@
     return mean, functools.reduce(jnp.add, spread) / count
 
 
+def grid_of(n):
+    side = 1 << ((n.bit_length() - 1) // 2)
+    return n // side, side
+
+
+def hops(n, i, j):
+    side = grid_of(n)[1]
+    return abs(i // side - j // side) + abs(i % side - j % side)
+
+
+def plan(n, middle):
+    lines, side = grid_of(n)
+    mine = [i for i in range(n) if (i // side in (lines // 2 - 1, lines // 2)) == middle]
+    reach = {d: max(hops(n, i, i ^ d) for i in mine) for d in range(1, n)}
+    inside = [d for d in range(side, n // 2)]
+    along = [d for d in range(1, side)]
+    across = sorted(range(n // 2, n), key=lambda d: (reach[d], d % side) if middle else (-(d // side), d % side))
+    return reach, inside, along, across
+
+
 def exchange(
     n, m, horizon, samples,
-    rewards, values, last, done, offset, rate_d, rate_t,
+    rewards, values, last_in, done_in, offset_in, rate_d_in, rate_t_in,
     out_a, out_v,
+    last, done, offset, rate_d, rate_t,
     p_buf, v_buf, d_buf, vt, at, src, summary, st_one, env_stats, st_two, tm_stats,
-    load_r, load_v, send_big, recv_v, recv_a, send_sum, recv_sum,
-    send_env, recv_env, send_tm, recv_tm,
+    load_small, load_r, load_v, send_big, recv_v, recv_a, send_sum, recv_sum,
+    send_env, recv_env, send_tm, recv_tm, gates,
 ):
     steps, envs = v_buf.shape
     rows = envs // n
     part = steps // CHUNKS
     me = lax.axis_index("tm")
     my_env = lax.axis_index("env")
-    links = [(lax.rem(me + d, n), lax.rem(me + n - d, n)) for d in range(1, n)]
-    peers = [target for target, unused in links]
+    lines, side = grid_of(n)
+    line, spot = me // side, lax.rem(me, side)
+    middle = jnp.logical_or(line == lines // 2 - 1, line == lines // 2)
+    peers = [jnp.bitwise_xor(me, d) for d in range(1, n)]
     mates = [lax.rem(my_env + d, m) for d in range(1, m)]
 
+    neighbours = [
+        (line > 0, me - side),
+        (line < lines - 1, me + side),
+        (spot > 0, me - 1),
+        (spot < side - 1, me + 1),
+    ]
+    near = functools.reduce(jnp.add, [there.astype(jnp.int32) for there, unused in neighbours])
+
+    def announce(sem):
+        for there, peer in neighbours:
+            @pl.when(there)
+            def unused_tell():
+                pl.semaphore_signal(sem, inc=1, device_id={"tm": peer}, device_id_type=MESH)
+
+    barrier = pltpu.get_barrier_semaphore()
+    for mate in mates:
+        pl.semaphore_signal(barrier, inc=1, device_id={"env": mate}, device_id_type=MESH)
+    announce(barrier)
+
+    cuts = [(0, SIDE), (SIDE, part - SIDE)] + [(c * part, part) for c in range(1, CHUNKS)]
     loads_v = [
         pltpu.make_async_copy(
-            values.at[pl.ds(c * part, part)], v_buf.at[pl.ds(c * part, part)], load_v.at[c]
+            values.at[pl.ds(t, size)], v_buf.at[pl.ds(t, size)], load_v.at[c]
         )
-        for c in range(CHUNKS)
+        for c, (t, size) in enumerate(cuts)
     ]
     loading_r = pltpu.make_async_copy(rewards, p_buf, load_r)
-    for load in loads_v:
+    loads_small = [
+        pltpu.make_async_copy(source, target, load_small.at[i])
+        for i, (source, target) in enumerate(
+            ((done_in, done), (offset_in, offset), (rate_d_in, rate_d), (rate_t_in, rate_t), (last_in, last))
+        )
+    ]
+    for load in loads_v + loads_small + [loading_r]:
         load.start()
-    loading_r.start()
-
-    barrier = pltpu.get_barrier_semaphore()
-    for peer in peers:
-        pl.semaphore_signal(barrier, inc=1, device_id={"tm": peer}, device_id_type=MESH)
-    for mate in mates:
-        pl.semaphore_signal(barrier, inc=1, device_id={"env": mate}, device_id_type=MESH)
-    pl.semaphore_wait(barrier, n + m - 2)
-
-    def send_part(which, source, target, sems, first, width, places):
-        for place in places:
-            peer = links[place][0]
-            pltpu.make_async_remote_copy(
-                src_ref=source.at[
-                    pl.ds(pl.multiple_of(peer * rows, 8), rows), pl.ds(first, width)
-                ],
-                dst_ref=target.at[
-                    pl.ds(0, rows), pl.ds(pl.multiple_of(me * steps + first, SIDE), width)
-                ],
-                send_sem=send_big.at[which],
-                recv_sem=sems(place),
-                device_id={"tm": peer},
-                device_id_type=MESH,
-            ).start()
-
-    everyone = range(n - 1)
-
-    def send_values(first, width):
-        send_part(0, vt, out_v, lambda place: recv_v.at[place], first, width, everyone)
-
-    def send_advantages(c, places):
-        sems = lambda place: recv_a.at[place * CHUNKS + c]
-        send_part(1, at, out_a, sems, c * part, part, places)
+
+    def send_part(which, source, target, sem, first, width, d):
+        peer = peers[d - 1]
+        pltpu.make_async_remote_copy(
+            src_ref=source.at[
+                pl.ds(pl.multiple_of(peer * rows, 8), rows), pl.ds(first, width)
+            ],
+            dst_ref=target.at[
+                pl.ds(0, rows), pl.ds(pl.multiple_of(me * steps + first, SIDE), width)
+            ],
+            send_sem=send_big.at[which],
+            recv_sem=sem,
+            device_id={"tm": peer},
+            device_id_type=MESH,
+        ).start()
+
+    def send_values(first, width, d):
+        send_part(0, vt, out_v, recv_v.at[d - 1], first, width, d)
+
+    def send_advantages(c, d):
+        send_part(1, at, out_a, recv_a.at[(d - 1) * CHUNKS + c], c * part, part, d)
+
+    def by_role(body):
+        @pl.when(middle)
+        def unused_middle():
+            body(True, *plan(n, True))
+
+        @pl.when(jnp.logical_not(middle))
+        def unused_end():
+            body(False, *plan(n, False))
 
     def turn_values(first, width):
         def body(b, unused):
@@ -89,26 +136,47 @@
 
         lax.fori_loop(0, width // SIDE, body, 0)
 
-    half = CHUNKS // 2
-    loads_v[0].wait()
-    turn_values(0, SIDE)
-    send_values(0, SIDE)
-    turn_values(SIDE, part - SIDE)
-    send_values(SIDE, part - SIDE)
-    for c in range(1, half):
-        loads_v[c].wait()
-        turn_values(c * part, part)
-        send_values(c * part, part)
-    for c in range(half, CHUNKS):
-        loads_v[c].wait()
+    for load, (t, size) in zip(loads_v[:2], cuts[:2]):
+        load.wait()
+        turn_values(t, size)
+    pl.semaphore_wait(barrier, near + m - 1)
+
+    farthest = lines + side - 2
+    for k in range(1, farthest + 1):
+        if k > 1:
+            pl.semaphore_wait(gates.at[k - 2], near)
+        if k < farthest:
+            announce(gates.at[k - 1])
+
+        def first_sends(middle, reach, inside, along, across):
+            for d in inside + across + along:
+                if reach[d] == k:
+                    for t, size in cuts[:2]:
+                        send_values(t, size, d)
+
+        by_role(first_sends)
+        if k == 1:
+            loads_v[2].wait()
+            turn_values(part, part)
+
+    def second_sends(middle, reach, inside, along, across):
+        if middle:
+            for d in across[: len(across) // 2]:
+                send_values(part, part, d)
+
+    by_role(second_sends)
+    for c in range(2, CHUNKS):
+        loads_v[c + 1].wait()
     loading_r.wait()
+    for load in loads_small:
+        load.wait()
 
     discount = jnp.exp(-rate_d[...])
     retention = discount * jnp.exp(-rate_t[...])
     first = me * steps
     wide = (8, envs)
     ends = [jnp.broadcast_to(done[j : j + 1, :] - first, wide) for j in range(done.shape[0])]
-    cuts = [
+    resets = [
         jnp.broadcast_to(k * horizon - 1 - first - offset[...], wide)
         for k in (1, 2)
     ]
@@ -123,7 +191,7 @@
         r = p_buf[at_rows, :]
         moment = row + k * 8
         finished = functools.reduce(jnp.logical_or, [moment == e for e in ends])
-        stopped = functools.reduce(jnp.logical_or, [moment == e for e in cuts], finished)
+        stopped = functools.reduce(jnp.logical_or, [moment == e for e in resets], finished)
         reach = jnp.where(finished, 0.0, disc)
         decay = jnp.where(stopped, 0.0, keep)
         v_up = pltpu.roll(v, 7, 0)
@@ -159,15 +227,22 @@
     src[1:2, :] = d_buf[0:1, :]
     src[2:3, :] = v_buf[0:1, :]
     src[5:8, :] = jnp.zeros((3, envs), jnp.float32)
-    turn_values(half * part, steps - half * part)
     summary[me] = src[...]
     for peer in peers:
         pltpu.make_async_remote_copy(
             src_ref=src, dst_ref=summary.at[me], send_sem=send_sum, recv_sem=recv_sum,
             device_id={"tm": peer}, device_id_type=MESH,
         ).start()
-    for c in range(half, CHUNKS):
-        send_values(c * part, part)
+    turn_values(2 * part, steps - 2 * part)
+
+    def other_sends(middle, reach, inside, along, across):
+        early = across[: len(across) // 2] if middle else []
+        for c in range(1, CHUNKS):
+            for d in inside + along + across:
+                if c > 1 or d not in early:
+                    send_values(c * part, part, d)
+
+    by_role(other_sends)
 
     def wait_all(source_like, sem):
         pltpu.make_async_copy(source_like, source_like, sem).wait()
@@ -235,8 +310,15 @@
             src_ref=st_one, dst_ref=env_stats.at[my_env], send_sem=send_env, recv_sem=recv_env,
             device_id={"env": mate}, device_id_type=MESH,
         ).start()
-    send_advantages(0, everyone)
-    send_advantages(1, everyone)
+    def advantage_sends(chunks):
+        def body(middle, reach, inside, along, across):
+            for c in chunks:
+                for d in inside + along + across:
+                    send_advantages(c, d)
+
+        by_role(body)
+
+    advantage_sends((0, 1))
     wait_all(env_stats.at[pl.ds(0, m - 1)], recv_env)
     mean, var = combine([env_stats[q] for q in range(m)])
     st_two[0:2, :] = mean
@@ -248,8 +330,7 @@
             src_ref=st_two, dst_ref=tm_stats.at[me], send_sem=send_tm, recv_sem=recv_tm,
             device_id={"tm": peer}, device_id_type=MESH,
         ).start()
-    for c in range(2, CHUNKS):
-        send_advantages(c, everyone)
+    advantage_sends(range(2, CHUNKS))
 
     wait_all(tm_stats.at[pl.ds(0, n - 1)], recv_tm)
     mean, var = combine([tm_stats[q] for q in range(n)])
@@ -279,7 +360,7 @@
     lax.fori_loop(0, CHUNKS, own, 0)
 
     def arrived(place, c):
-        first = pl.multiple_of(links[place][1] * steps + c * part, SIDE)
+        first = pl.multiple_of(peers[place] * steps + c * part, SIDE)
         piece = out_a.at[:, pl.ds(0, part)]
         if c == 0:
             wait_all(out_v.at[:, pl.ds(0, steps)], recv_v.at[place])
@@ -287,15 +368,43 @@
         read = lambda source: lambda r: source[pl.ds(r, 8), pl.ds(first, part)]
         normalize(read(out_a), read(out_v), first)
 
+    unused_reach, inside, along, across = plan(n, True)
     for c in range(CHUNKS):
-        for place in everyone:
-            arrived(place, c)
+        for d in inside + along + across[::-1]:
+            arrived(d - 1, c)
 
     wait_all(others, send_sum)
     wait_all(env_stats.at[pl.ds(0, m - 1)], send_env)
     wait_all(tm_stats.at[pl.ds(0, n - 1)], send_tm)
     for which, source in enumerate((vt, at)):
         wait_all(source.at[pl.ds(0, (n - 1) * rows)], send_big.at[which])
+
+
+def drain_kernel(a, v, out_a, out_v, sems):
+    part = a.shape[0] // PIECES
+    copies = [
+        pltpu.make_async_copy(source.at[pl.ds(i * part, part)], target.at[pl.ds(i * part, part)], sems.at[k, i])
+        for i in range(PIECES)
+        for k, (source, target) in enumerate(((a, out_a), (v, out_v)))
+    ]
+    for copy in copies:
+        copy.start()
+    for copy in copies:
+        copy.wait()
+
+
+def drain(a, v):
+    shape = jax.ShapeDtypeStruct(a.shape, a.dtype)
+    local = pl.BlockSpec(memory_space=pltpu.VMEM)
+    remote = pl.BlockSpec(memory_space=pltpu.HBM)
+    return pl.pallas_call(
+        drain_kernel,
+        out_shape=(shape, shape),
+        in_specs=(local, local),
+        out_specs=(remote, remote),
+        scratch_shapes=[pltpu.SemaphoreType.DMA((2, PIECES))],
+        compiler_params=pltpu.CompilerParams(vmem_limit_bytes=1024 * 1024),
+    )(a, v)
 
 
 def shards(rewards, values, last_value, done_steps, horizon_offset, discount_rate, trace_rate):
@@ -309,12 +418,17 @@
     local = pl.BlockSpec(memory_space=pltpu.VMEM)
     f32 = jnp.float32
     dma = pltpu.SemaphoreType.DMA
-    return pl.pallas_call(
+    a, v = pl.pallas_call(
         kernel,
         out_shape=(whole, whole),
-        in_specs=[remote] * 2 + [local] * 5,
+        in_specs=[remote] * 7,
         out_specs=(local, local),
         scratch_shapes=[
+            pltpu.VMEM((1, envs), f32),
+            pltpu.VMEM(done_steps.shape[::-1], jnp.int32),
+            pltpu.VMEM((1, envs), jnp.int32),
+            pltpu.VMEM((1, envs), f32),
+            pltpu.VMEM((1, envs), f32),
             pltpu.VMEM((steps, envs), f32),
             pltpu.VMEM((steps, envs), f32),
             pltpu.VMEM((steps, envs), f32),
@@ -326,8 +440,8 @@
             pltpu.VMEM((m, 8, SIDE), f32),
             pltpu.VMEM((8, SIDE), f32),
             pltpu.VMEM((n, 8, SIDE), f32),
-            dma, dma((CHUNKS,)), dma((2,)), dma((n - 1,)), dma(((n - 1) * CHUNKS,)), dma, dma,
-            dma, dma, dma, dma,
+            dma((5,)), dma, dma((CHUNKS + 1,)), dma((2,)), dma((n - 1,)), dma(((n - 1) * CHUNKS,)), dma, dma,
+            dma, dma, dma, dma, pltpu.SemaphoreType.REGULAR((n,)),
         ],
         compiler_params=pltpu.CompilerParams(
             collective_id=0, has_side_effects=True, vmem_limit_bytes=55 * 1024 * 1024
@@ -341,6 +455,7 @@
         discount_rate[None, :],
         trace_rate[None, :],
     )
+    return drain(a, v)
 
 
 def solution(mesh):

time: 194 us -> 196 us (1.010)
  the two profiles are of different devices: /device:TPU:15 before, /device:TPU:0 now
where the time goes in v1:
time: 196 us
  Pallas kernels  195 us (99%)
    pallas_call x1, Pallas kernels, shards(): pl.pallas_call(kernel, out_shape=(whole, whole), in_specs=[remote] * 7, o...  192 us

profile of v1, /device:TPU:0, one launch (start us, length us, event | category | flops | bytes accessed | tf_op | source)
XLA Modules:
  0.0 196.1 jit_solution(8095096493606343851)
XLA Ops:
  0.6 192.1 %shard_map.86 = (f32[64,16384]{1,0:T(8,128)S(1)}, f32[64,16384]{1,0:T(8,128)S(1)}) custom-call(f32[2048,512]{1,0:T(8,128)} %rewards.1, f32[2048,512]{1,0:T(8,128)} %values.1, f32[1,512]{1,0:T(1,128)} %bitcast.6, s32[4,512]{1,0:T(4,128)} %bitcast.5, s32[1,512]{1,0:T(1,128)} %bitcast.7, f32[1,512]{1,0:T(1,128)} %bitcast.8, f32[1,512]{1,0:T(1,128)} %bitcast.9), custom_call_target="tpu_custom_call" | custom-call | tf_op jit(solution)/shard_map/pallas_call | solution.py:421
  192.8 3.4 %shard_map.87 = (f32[64,16384]{1,0:T(8,128)}, f32[64,16384]{1,0:T(8,128)}) custom-call(f32[64,16384]{1,0:T(8,128)S(1)} %get-tuple-element.4.a, f32[64,16384]{1,0:T(8,128)S(1)} %get-tuple-element.5.v), custom_call_target="tpu_custom_call" | custom-call | tf_op jit(solution)/shard_map/pallas_call | solution.py:400

commit v2 on v1

--- a/solution.py
+++ b/solution.py
@@ -11,6 +11,8 @@
 CHUNKS = 4
 SIDE = 128
 PIECES = 4
+HELD = 1
+HELD_TILL = 3
 
 
 def combine(parts):
@@ -314,7 +316,8 @@
         def body(middle, reach, inside, along, across):
             for c in chunks:
                 for d in inside + along + across:
-                    send_advantages(c, d)
+                    if not (middle and d in across and c >= CHUNKS - HELD):
+                        send_advantages(c, d)
 
         by_role(body)
 
@@ -359,19 +362,33 @@
 
     lax.fori_loop(0, CHUNKS, own, 0)
 
-    def arrived(place, c):
-        first = pl.multiple_of(peers[place] * steps + c * part, SIDE)
-        piece = out_a.at[:, pl.ds(0, part)]
+    def landed(place, c):
         if c == 0:
             wait_all(out_v.at[:, pl.ds(0, steps)], recv_v.at[place])
-        wait_all(piece, recv_a.at[place * CHUNKS + c])
+        wait_all(out_a.at[:, pl.ds(0, part)], recv_a.at[place * CHUNKS + c])
+
+    def arrived(place, c, waited):
+        first = pl.multiple_of(peers[place] * steps + c * part, SIDE)
+        if not waited:
+            landed(place, c)
         read = lambda source: lambda r: source[pl.ds(r, 8), pl.ds(first, part)]
         normalize(read(out_a), read(out_v), first)
 
     unused_reach, inside, along, across = plan(n, True)
+    far = [d for d in across if lines // 2 <= d // side < lines - 1]
+    for c in range(HELD_TILL):
+        for d in far:
+            landed(d - 1, c)
+
+    @pl.when(middle)
+    def unused_held():
+        for c in range(CHUNKS - HELD, CHUNKS):
+            for d in across[::-1]:
+                send_advantages(c, d)
+
     for c in range(CHUNKS):
         for d in inside + along + across[::-1]:
-            arrived(d - 1, c)
+            arrived(d - 1, c, d in far and c < HELD_TILL)
 
     wait_all(others, send_sum)
     wait_all(env_stats.at[pl.ds(0, m - 1)], send_env)

time: 196 us -> 193 us (0.985)
  Pallas kernels: 195 us -> 192 us
    pallas_call x1, Pallas kernels: 192 us -> 189 us  [shards(): pl.pallas_call(kernel, out_shape=(whole, whole), in_specs=[remote] * 7, o...]
where the time goes in v2:
time: 193 us
  Pallas kernels  192 us (99%)
    pallas_call x1, Pallas kernels, shards(): pl.pallas_call(kernel, out_shape=(whole, whole), in_specs=[remote] * 7, o...  189 us

profile of v2, /device:TPU:0, one launch (start us, length us, event | category | flops | bytes accessed | tf_op | source)
XLA Modules:
  0.0 192.8 jit_solution(6469993394707755482)
XLA Ops:
  0.6 188.8 %shard_map.86 = (f32[64,16384]{1,0:T(8,128)S(1)}, f32[64,16384]{1,0:T(8,128)S(1)}) custom-call(f32[2048,512]{1,0:T(8,128)} %rewards.1, f32[2048,512]{1,0:T(8,128)} %values.1, f32[1,512]{1,0:T(1,128)} %bitcast.6, s32[4,512]{1,0:T(4,128)} %bitcast.5, s32[1,512]{1,0:T(1,128)} %bitcast.7, f32[1,512]{1,0:T(1,128)} %bitcast.8, f32[1,512]{1,0:T(1,128)} %bitcast.9), custom_call_target="tpu_custom_call" | custom-call | tf_op jit(solution)/shard_map/pallas_call | solution.py:438
  189.5 3.4 %shard_map.87 = (f32[64,16384]{1,0:T(8,128)}, f32[64,16384]{1,0:T(8,128)}) custom-call(f32[64,16384]{1,0:T(8,128)S(1)} %get-tuple-element.4.a, f32[64,16384]{1,0:T(8,128)S(1)} %get-tuple-element.5.v), custom_call_target="tpu_custom_call" | custom-call | tf_op jit(solution)/shard_map/pallas_call | solution.py:417

commit v3 on v2

--- a/solution.py
+++ b/solution.py
@@ -12,14 +12,15 @@
 SIDE = 128
 PIECES = 4
 HELD = 1
-HELD_TILL = 3
+HELD_TILL = 2
+EARLY = 2
 
 
 def combine(parts):
     count = len(parts)
-    means = [part[0:2] for part in parts]
+    means = [part[0:1] for part in parts]
     mean = functools.reduce(jnp.add, means) / count
-    spread = [part[2:4] + (m - mean) * (m - mean) for part, m in zip(parts, means)]
+    spread = [part[1:2] + (m - mean) * (m - mean) for part, m in zip(parts, means)]
     return mean, functools.reduce(jnp.add, spread) / count
 
 
@@ -48,8 +49,8 @@
     rewards, values, last_in, done_in, offset_in, rate_d_in, rate_t_in,
     out_a, out_v,
     last, done, offset, rate_d, rate_t,
-    p_buf, v_buf, d_buf, vt, at, src, summary, st_one, env_stats, st_two, tm_stats,
-    load_small, load_r, load_v, send_big, recv_v, recv_a, send_sum, recv_sum,
+    p_buf, v_buf, d_buf, vt, at, src, summary, border, entry, st_one, env_stats, st_two, tm_stats,
+    load_small, load_r, load_v, send_big, recv_v, recv_a, send_sum, recv_sum, send_border, recv_border,
     send_env, recv_env, send_tm, recv_tm, gates,
 ):
     steps, envs = v_buf.shape
@@ -151,7 +152,7 @@
             announce(gates.at[k - 1])
 
         def first_sends(middle, reach, inside, along, across):
-            for d in inside + across + along:
+            for d in inside + (across if middle else []) + along:
                 if reach[d] == k:
                     for t, size in cuts[:2]:
                         send_values(t, size, d)
@@ -162,9 +163,8 @@
             turn_values(part, part)
 
     def second_sends(middle, reach, inside, along, across):
-        if middle:
-            for d in across[: len(across) // 2]:
-                send_values(part, part, d)
+        for d in across[:EARLY] if middle else inside + along:
+            send_values(part, part, d)
 
     by_role(second_sends)
     for c in range(2, CHUNKS):
@@ -229,38 +229,76 @@
     src[1:2, :] = d_buf[0:1, :]
     src[2:3, :] = v_buf[0:1, :]
     src[5:8, :] = jnp.zeros((3, envs), jnp.float32)
-    summary[me] = src[...]
-    for peer in peers:
+    half = n // 2
+    place = lax.rem(me, half)
+    later = me >= half
+    summary[place] = src[...]
+    for d in range(1, half):
         pltpu.make_async_remote_copy(
-            src_ref=src, dst_ref=summary.at[me], send_sem=send_sum, recv_sem=recv_sum,
-            device_id={"tm": peer}, device_id_type=MESH,
+            src_ref=src, dst_ref=summary.at[place], send_sem=send_sum, recv_sem=recv_sum,
+            device_id={"tm": peers[d - 1]}, device_id_type=MESH,
         ).start()
-    turn_values(2 * part, steps - 2 * part)
 
     def other_sends(middle, reach, inside, along, across):
-        early = across[: len(across) // 2] if middle else []
-        for c in range(1, CHUNKS):
-            for d in inside + along + across:
-                if c > 1 or d not in early:
+        for c in range(CHUNKS):
+            near_by = inside + along
+            if c < (1 if middle else 2):
+                near_by = []
+            far_side = across
+            if middle and c == 0:
+                far_side = []
+            if middle and c == 1:
+                far_side = across[EARLY:]
+            for d in near_by + far_side:
+                if c == 0:
+                    for t, size in cuts[:2]:
+                        send_values(t, size, d)
+                else:
                     send_values(c * part, part, d)
-
-    by_role(other_sends)
 
     def wait_all(source_like, sem):
         pltpu.make_async_copy(source_like, source_like, sem).wait()
 
-    others = summary.at[pl.ds(0, n - 1)]
+    turn_values(2 * part, steps - 2 * part)
+
+    @pl.when(jnp.logical_not(later))
+    def unused_send_early():
+        by_role(other_sends)
+
+    others = summary.at[pl.ds(0, half - 1)]
     wait_all(others, recv_sum)
 
-    a_next = jnp.zeros((1, envs), jnp.float32)
-    v_next = last[...]
+    crossing = pltpu.make_async_remote_copy(
+        src_ref=border, dst_ref=entry, send_sem=send_border, recv_sem=recv_border,
+        device_id={"tm": peers[half - 1]}, device_id_type=MESH,
+    )
+
+    @pl.when(later)
+    def unused_last():
+        entry[0:1, :] = jnp.zeros((1, envs), jnp.float32)
+        entry[1:2, :] = last[...]
+
+    @pl.when(jnp.logical_not(later))
+    def unused_entry():
+        crossing.wait_recv()
+
+    a_next = entry[0:1, :]
+    v_next = entry[1:2, :]
     lift = jnp.zeros((1, envs), jnp.float32)
-    for p in reversed(range(n)):
+    for p in reversed(range(half)):
         block = summary[p]
         added = block[3:4] * v_next + block[4:5] * a_next
-        lift = jnp.where(me == p, added, lift)
+        lift = jnp.where(place == p, added, lift)
         a_next = block[0:1] + block[1:2] * added
         v_next = block[2:3]
+    border[0:1, :] = a_next
+    border[1:2, :] = v_next
+
+    @pl.when(later)
+    def unused_cross():
+        crossing.start()
+        by_role(other_sends)
+
     src_lift = [jnp.broadcast_to(lift[:, e : e + SIDE], (SIDE, SIDE)) for e in range(0, envs, SIDE)]
 
     def fold(x):
@@ -300,11 +338,13 @@
     zero = jnp.zeros((8, span), jnp.float32)
     sq_a, sq_r = lax.fori_loop(0, envs // 8, squares, (zero, zero))
     lane = (1, SIDE)
-    st_one[0:1, :] = jnp.broadcast_to(mean_a, lane)
-    st_one[1:2, :] = jnp.broadcast_to(mean_r, lane)
-    st_one[2:3, :] = jnp.broadcast_to(total(sq_a) / samples, lane)
-    st_one[3:4, :] = jnp.broadcast_to(total(sq_r) / samples, lane)
-    st_one[4:8, :] = jnp.zeros((4, SIDE), jnp.float32)
+    is_a = lax.broadcasted_iota(jnp.int32, lane, 1) < SIDE // 2
+
+    def both(a, r):
+        return jnp.where(is_a, jnp.broadcast_to(a, lane), jnp.broadcast_to(r, lane))
+
+    st_one[0:1, :] = both(mean_a, mean_r)
+    st_one[1:2, :] = both(total(sq_a) / samples, total(sq_r) / samples)
     env_stats[my_env] = st_one[...]
 
     for mate in mates:
@@ -324,9 +364,8 @@
     advantage_sends((0, 1))
     wait_all(env_stats.at[pl.ds(0, m - 1)], recv_env)
     mean, var = combine([env_stats[q] for q in range(m)])
-    st_two[0:2, :] = mean
-    st_two[2:4, :] = var
-    st_two[4:8, :] = jnp.zeros((4, SIDE), jnp.float32)
+    st_two[0:1, :] = mean
+    st_two[1:2, :] = var
     tm_stats[me] = st_two[...]
     for peer in peers:
         pltpu.make_async_remote_copy(
@@ -340,7 +379,7 @@
     scale = lax.rsqrt(var + 1e-05)
     wide = (8, part)
     mid_a, mid_r, scale_a, scale_r = (
-        jnp.broadcast_to(x[i : i + 1, 0:1], wide) for x in (mean, scale) for i in (0, 1)
+        jnp.broadcast_to(x[0:1, i : i + 1], wide) for x in (mean, scale) for i in (0, SIDE // 2)
     )
 
     def normalize(read_a, read_v, first):
@@ -391,6 +430,11 @@
             arrived(d - 1, c, d in far and c < HELD_TILL)
 
     wait_all(others, send_sum)
+
+    @pl.when(later)
+    def unused_crossed():
+        crossing.wait_send()
+
     wait_all(env_stats.at[pl.ds(0, m - 1)], send_env)
     wait_all(tm_stats.at[pl.ds(0, n - 1)], send_tm)
     for which, source in enumerate((vt, at)):
@@ -452,13 +496,15 @@
             pltpu.VMEM((envs, steps), f32),
             pltpu.VMEM((envs, steps), f32),
             pltpu.VMEM((8, envs), f32),
-            pltpu.VMEM((n, 8, envs), f32),
-            pltpu.VMEM((8, SIDE), f32),
-            pltpu.VMEM((m, 8, SIDE), f32),
-            pltpu.VMEM((8, SIDE), f32),
-            pltpu.VMEM((n, 8, SIDE), f32),
+            pltpu.VMEM((n // 2, 8, envs), f32),
+            pltpu.VMEM((2, envs), f32),
+            pltpu.VMEM((2, envs), f32),
+            pltpu.VMEM((2, SIDE), f32),
+            pltpu.VMEM((m, 2, SIDE), f32),
+            pltpu.VMEM((2, SIDE), f32),
+            pltpu.VMEM((n, 2, SIDE), f32),
             dma((5,)), dma, dma((CHUNKS + 1,)), dma((2,)), dma((n - 1,)), dma(((n - 1) * CHUNKS,)), dma, dma,
-            dma, dma, dma, dma, pltpu.SemaphoreType.REGULAR((n,)),
+            dma, dma, dma, dma, dma, dma, pltpu.SemaphoreType.REGULAR((n,)),
         ],
         compiler_params=pltpu.CompilerParams(
             collective_id=0, has_side_effects=True, vmem_limit_bytes=55 * 1024 * 1024

time: 193 us -> 190 us (0.984)
  Pallas kernels: 192 us -> 190 us
    pallas_call x1, Pallas kernels: 189 us -> 186 us  [shards(): pl.pallas_call(kernel, out_shape=(whole, whole), in_specs=[remote] * 7, o...]
where the time goes in v3:
time: 190 us
  Pallas kernels  190 us (100%)
    pallas_call x1, Pallas kernels, shards(): pl.pallas_call(kernel, out_shape=(whole, whole), in_specs=[remote] * 7, o...  186 us

profile of v3, /device:TPU:0, one launch (start us, length us, event | category | flops | bytes accessed | tf_op | source)
XLA Modules:
  0.0 190.3 jit_solution(2005775691651303709)
XLA Ops:
  0.6 186.3 %shard_map.86 = (f32[64,16384]{1,0:T(8,128)S(1)}, f32[64,16384]{1,0:T(8,128)S(1)}) custom-call(f32[2048,512]{1,0:T(8,128)} %rewards.1, f32[2048,512]{1,0:T(8,128)} %values.1, f32[1,512]{1,0:T(1,128)} %bitcast.6, s32[4,512]{1,0:T(4,128)} %bitcast.5, s32[1,512]{1,0:T(1,128)} %bitcast.7, f32[1,512]{1,0:T(1,128)} %bitcast.8, f32[1,512]{1,0:T(1,128)} %bitcast.9), custom_call_target="tpu_custom_call" | custom-call | tf_op jit(solution)/shard_map/pallas_call | solution.py:482
  186.9 3.4 %shard_map.87 = (f32[64,16384]{1,0:T(8,128)}, f32[64,16384]{1,0:T(8,128)}) custom-call(f32[64,16384]{1,0:T(8,128)S(1)} %get-tuple-element.4.a, f32[64,16384]{1,0:T(8,128)S(1)} %get-tuple-element.5.v), custom_call_target="tpu_custom_call" | custom-call | tf_op jit(solution)/shard_map/pallas_call | solution.py:461

commit v4 on v3

--- a/solution.py
+++ b/solution.py
@@ -11,8 +11,6 @@
 CHUNKS = 4
 SIDE = 128
 PIECES = 4
-HELD = 1
-HELD_TILL = 2
 EARLY = 2
 
 
@@ -40,7 +38,7 @@
     reach = {d: max(hops(n, i, i ^ d) for i in mine) for d in range(1, n)}
     inside = [d for d in range(side, n // 2)]
     along = [d for d in range(1, side)]
-    across = sorted(range(n // 2, n), key=lambda d: (reach[d], d % side) if middle else (-(d // side), d % side))
+    across = sorted(range(n // 2, n), key=lambda d: (d // side, -(d % side)) if middle else -d)
     return reach, inside, along, across
 
 
@@ -356,8 +354,7 @@
         def body(middle, reach, inside, along, across):
             for c in chunks:
                 for d in inside + along + across:
-                    if not (middle and d in across and c >= CHUNKS - HELD):
-                        send_advantages(c, d)
+                    send_advantages(c, d)
 
         by_role(body)
 
@@ -401,33 +398,18 @@
 
     lax.fori_loop(0, CHUNKS, own, 0)
 
-    def landed(place, c):
+    def arrived(place, c):
+        first = pl.multiple_of(peers[place] * steps + c * part, SIDE)
         if c == 0:
             wait_all(out_v.at[:, pl.ds(0, steps)], recv_v.at[place])
         wait_all(out_a.at[:, pl.ds(0, part)], recv_a.at[place * CHUNKS + c])
-
-    def arrived(place, c, waited):
-        first = pl.multiple_of(peers[place] * steps + c * part, SIDE)
-        if not waited:
-            landed(place, c)
         read = lambda source: lambda r: source[pl.ds(r, 8), pl.ds(first, part)]
         normalize(read(out_a), read(out_v), first)
 
     unused_reach, inside, along, across = plan(n, True)
-    far = [d for d in across if lines // 2 <= d // side < lines - 1]
-    for c in range(HELD_TILL):
-        for d in far:
-            landed(d - 1, c)
-
-    @pl.when(middle)
-    def unused_held():
-        for c in range(CHUNKS - HELD, CHUNKS):
-            for d in across[::-1]:
-                send_advantages(c, d)
-
     for c in range(CHUNKS):
-        for d in inside + along + across[::-1]:
-            arrived(d - 1, c, d in far and c < HELD_TILL)
+        for d in inside + along + across:
+            arrived(d - 1, c)
 
     wait_all(others, send_sum)
 

time: 190 us -> 189 us (level); the launches traced: 190 us -> 187 us
  Pallas kernels: 190 us -> 186 us
    pallas_call x1, Pallas kernels: 186 us -> 183 us  [shards(): pl.pallas_call(kernel, out_shape=(whole, whole), in_specs=[remote] * 7, o...]
where the time goes in v4:
time: 189 us; the launch traced here: 187 us
  Pallas kernels  186 us (98%)
    pallas_call x1, Pallas kernels, shards(): pl.pallas_call(kernel, out_shape=(whole, whole), in_specs=[remote] * 7, o...  183 us

profile of v4, /device:TPU:0, one launch (start us, length us, event | category | flops | bytes accessed | tf_op | source)
XLA Modules:
  0.0 186.8 jit_solution(6473926271081515207)
XLA Ops:
  0.6 182.8 %shard_map.86 = (f32[64,16384]{1,0:T(8,128)S(1)}, f32[64,16384]{1,0:T(8,128)S(1)}) custom-call(f32[2048,512]{1,0:T(8,128)} %rewards.1, f32[2048,512]{1,0:T(8,128)} %values.1, f32[1,512]{1,0:T(1,128)} %bitcast.6, s32[4,512]{1,0:T(4,128)} %bitcast.5, s32[1,512]{1,0:T(1,128)} %bitcast.7, f32[1,512]{1,0:T(1,128)} %bitcast.8, f32[1,512]{1,0:T(1,128)} %bitcast.9), custom_call_target="tpu_custom_call" | custom-call | tf_op jit(solution)/shard_map/pallas_call | solution.py:464
  183.4 3.4 %shard_map.87 = (f32[64,16384]{1,0:T(8,128)}, f32[64,16384]{1,0:T(8,128)}) custom-call(f32[64,16384]{1,0:T(8,128)S(1)} %get-tuple-element.4.a, f32[64,16384]{1,0:T(8,128)S(1)} %get-tuple-element.5.v), custom_call_target="tpu_custom_call" | custom-call | tf_op jit(solution)/shard_map/pallas_call | solution.py:443

commit v5 on v4

--- a/solution.py
+++ b/solution.py
@@ -251,8 +251,10 @@
                 if c == 0:
                     for t, size in cuts[:2]:
                         send_values(t, size, d)
-                else:
-                    send_values(c * part, part, d)
+                elif c == 1:
+                    send_values(part, part, d)
+                elif c == 2:
+                    send_values(c * part, (CHUNKS - c) * part, d)
 
     def wait_all(source_like, sem):
         pltpu.make_async_copy(source_like, source_like, sem).wait()
@@ -353,7 +355,7 @@
     def advantage_sends(chunks):
         def body(middle, reach, inside, along, across):
             for c in chunks:
-                for d in inside + along + across:
+                for d in along + inside + across:
                     send_advantages(c, d)
 
         by_role(body)

time: 189 us -> 189 us (level)
  no operation moved by 1% of the time
where the time goes in v5:
time: 189 us; the launch traced here: 187 us
  Pallas kernels  186 us (98%)
    pallas_call x1, Pallas kernels, shards(): pl.pallas_call(kernel, out_shape=(whole, whole), in_specs=[remote] * 7, o...  183 us

profile of v5, /device:TPU:0, one launch (start us, length us, event | category | flops | bytes accessed | tf_op | source)
XLA Modules:
  0.0 186.7 jit_solution(10763062094603308166)
XLA Ops:
  0.6 182.7 %shard_map.86 = (f32[64,16384]{1,0:T(8,128)S(1)}, f32[64,16384]{1,0:T(8,128)S(1)}) custom-call(f32[2048,512]{1,0:T(8,128)} %rewards.1, f32[2048,512]{1,0:T(8,128)} %values.1, f32[1,512]{1,0:T(1,128)} %bitcast.6, s32[4,512]{1,0:T(4,128)} %bitcast.5, s32[1,512]{1,0:T(1,128)} %bitcast.7, f32[1,512]{1,0:T(1,128)} %bitcast.8, f32[1,512]{1,0:T(1,128)} %bitcast.9), custom_call_target="tpu_custom_call" | custom-call | tf_op jit(solution)/shard_map/pallas_call | solution.py:466
  183.4 3.4 %shard_map.87 = (f32[64,16384]{1,0:T(8,128)}, f32[64,16384]{1,0:T(8,128)}) custom-call(f32[64,16384]{1,0:T(8,128)S(1)} %get-tuple-element.4.a, f32[64,16384]{1,0:T(8,128)S(1)} %get-tuple-element.5.v), custom_call_target="tpu_custom_call" | custom-call | tf_op jit(solution)/shard_map/pallas_call | solution.py:445
